TPU v7x, 32 devices: a whole 2x2x4 slice. The times are simulated.
32 devices in a mesh: gx: 8 (over z, x), gy: 4 (over y, core).
Axes of the slice: x: 2, y: 2, z: 4, core: 2. Of those that a mesh axis runs over, the one named last changes fastest.
Arguments:
- populations: float32 [19, 64, 256, 256], P(None, 'gx', 'gy'), may hold values from 0 to 0.6
- rotation_init: float32 [3], replicated, may hold values from -0.75 to 0.75
- slot_cell: int32 [3, 8, 4, 2048], P(None, 'gx', 'gy'), may hold values from 0 to 255, as said below
- slot_count: int32 [8, 4], P('gx', 'gy'), may hold values from 128 to 2048, as said below
- marker_arm: float32 [3, 8, 4, 2048], P(None, 'gx', 'gy'), may hold values from -1.7 to 1.7
- marker_area: float32 [8, 4, 2048], P('gx', 'gy'), may hold values from 0.3 to 3
- marker_fraction: float32 [8, 4, 2048], P('gx', 'gy'), may hold values from 0 to 1
Outputs:
- populations_next: float32 [19, 64, 256, 256], P(None, 'gx', 'gy')
- rotation: float32 [3, 3], replicated
Inputs may be any that keep to these rules, and one draw needn't show every extreme that they name: `slot_cell`: slot s of slab (a, b) names a cell whose first coordinate lies in [a * 8, (a + 1) * 8) and whose second lies in [b * 64, (b + 1) * 64); the third is any; slots at or past slot_count hold cells too but carry no marker. `slot_count`: some slab has all 2048 slots live in every draw.
All inputs are finite; a program needn't handle non-finite values.
Results may differ from a plain program's by a relative error of at most 0.0001.
Values sent between devices are 32-bit elements; how exact they have to be, the bound alone decides.
A program may use at most 128 MiB of HBM per device.

v0:
```python
import functools

import jax
import jax.numpy as jnp
from jax import lax
from jax.experimental import pallas as pl
from jax.experimental.pallas import tpu as pltpu
from jax.sharding import PartitionSpec as P

Q = 19
ITERS = 3
VELOCITY_TABLE = (
    (0, 0, 0),
    (1, 0, 0),
    (-1, 0, 0),
    (0, 1, 0),
    (0, -1, 0),
    (0, 0, 1),
    (0, 0, -1),
    (1, 1, 0),
    (-1, -1, 0),
    (1, -1, 0),
    (-1, 1, 0),
    (1, 0, 1),
    (-1, 0, -1),
    (1, 0, -1),
    (-1, 0, 1),
    (0, 1, 1),
    (0, -1, -1),
    (0, 1, -1),
    (0, -1, 1),
)
WEIGHT_TABLE = (1.0 / 3.0,) + (1.0 / 18.0,) * 6 + (1.0 / 36.0,) * 12
RELAX_TIME = 0.8
SPREAD_GAIN = 0.25
SPIN_GAIN = 0.5
PLUS_X = [m for m in range(Q) if VELOCITY_TABLE[m][0] == 1]
MINUS_X = [m for m in range(Q) if VELOCITY_TABLE[m][0] == -1]
PLUS_Y = [m for m in range(Q) if VELOCITY_TABLE[m][1] == 1]
MINUS_Y = [m for m in range(Q) if VELOCITY_TABLE[m][1] == -1]
DIAGONAL = [m for m in range(Q) if VELOCITY_TABLE[m][0] != 0 and VELOCITY_TABLE[m][1] != 0]
MESH = pl.DeviceIdType.MESH
F32 = jnp.float32
BF16 = jnp.bfloat16
VMEM = pltpu.VMEM
VMEM_LIMIT = 60 * 1024 * 1024


def vmem():
    return pl.BlockSpec(memory_space=pltpu.VMEM)


def relax(member, value, density, velocity, common):
    direction = VELOCITY_TABLE[member]
    projected = None
    for number in range(3):
        if direction[number] != 0:
            term = velocity[number] if direction[number] > 0 else -velocity[number]
            projected = term if projected is None else projected + term
    scaled = density * (WEIGHT_TABLE[member] / RELAX_TIME)
    if projected is None:
        bracket = common
    else:
        bracket = common + projected * (3.0 + 4.5 * projected)
    return value * (1.0 - 1.0 / RELAX_TIME) + scaled * bracket


def common_of(velocity):
    squared = velocity[0] * velocity[0] + velocity[1] * velocity[1] + velocity[2] * velocity[2]
    return 1.0 - 1.5 * squared


def moments_kernel(pops_ref, density_ref, velocity_ref):
    depth = pops_ref.shape[3]
    values = [pops_ref[m, 0] for m in range(Q)]
    density = values[0]
    for m in range(1, Q):
        density = density + values[m]
    density_ref[...] = density
    for number in range(3):
        total = None
        for m in range(Q):
            direction = VELOCITY_TABLE[m][number]
            if direction != 0:
                if total is None:
                    total = values[m]
                else:
                    total = total + values[m] if direction > 0 else total - values[m]
        velocity_ref[:, number * depth : (number + 1) * depth] = total / density


def pieces_of(value, count):
    found = []
    for number in range(count):
        piece = value.astype(BF16)
        found.append(piece)
        if number < count - 1:
            value = value - piece.astype(F32)
    return found


def depth_table(depth, low, fraction):
    high = jnp.where(low == depth - 1.0, 0.0, low + 1.0)
    ids = lax.broadcasted_iota(jnp.int32, (depth, low.shape[1]), 0).astype(F32)
    return jnp.where(ids == low, 1.0 - fraction, 0.0) + jnp.where(ids == high, fraction, 0.0)


def plane_table(planes, row):
    ids = lax.broadcasted_iota(jnp.int32, (planes, row.shape[1]), 0).astype(F32)
    return jnp.where(ids == row, 1.0, 0.0).astype(BF16)


def gather_kernel(
    velocity_ref,
    pack_ref,
    sums_ref,
    linear_ref,
    turned_hi,
    turned_lo,
    state_ref,
    result_ref,
    cell_col,
    high_col,
    same_ref,
    after_ref,
    before_ref,
    left_ref,
):
    planes, triple = velocity_ref.shape
    depth = triple // 3
    slots = pack_ref.shape[1]
    turned = jnp.transpose(velocity_ref[...])
    hi, lo = pieces_of(turned, 2)
    turned_hi[...] = hi
    turned_lo[...] = lo
    chunk = 256
    steps = slots // chunk

    def gather(step, carry):
        at = pl.ds(pl.multiple_of(step * chunk, chunk), chunk)
        table = plane_table(planes, pack_ref[0:1, at])
        rows = jnp.dot(turned_hi[...], table, preferred_element_type=F32)
        rows = rows + jnp.dot(turned_lo[...], table, preferred_element_type=F32)
        tap = depth_table(depth, pack_ref[1:2, at], pack_ref[3:4, at])
        for number in range(3):
            part = rows[number * depth : (number + 1) * depth]
            state_ref[number : number + 1, at] = jnp.sum(part * tap, axis=0, keepdims=True)
        return carry

    lax.fori_loop(0, steps, gather, 0)
    state_ref[3:6, :] = pack_ref[4:7, :]
    state_ref[6:8, :] = jnp.zeros((2, slots), F32)

    low = pack_ref[1:2, :]
    high = jnp.where(low == depth - 1.0, 0.0, low + 1.0)
    base = pack_ref[0:1, :] * float(depth)
    cell_row = base + low
    high_row = base + high
    both = jnp.concatenate([cell_row, high_row, jnp.zeros((6, slots), F32)], axis=0)
    columns = jnp.transpose(both)
    cell_col[...] = jnp.broadcast_to(columns[:, 0:1], (slots, 128))
    high_col[...] = jnp.broadcast_to(columns[:, 1:2], (slots, 128))
    result_ref[6:8, :] = both[0:2]

    def prepare():
        weighted = state_ref[...] * pack_ref[2:3, :]
        share = pack_ref[3:4, :]
        stacked = jnp.concatenate([weighted * (1.0 - share), weighted * share], axis=0)
        left_ref[...] = jnp.concatenate(pieces_of(stacked, 3), axis=0)

    def apply(build):
        def one(step, carry):
            at = pl.ds(pl.multiple_of(step * chunk, chunk), chunk)
            if build:
                for half in range(chunk // 128):
                    part = pl.ds(pl.multiple_of(step * chunk + half * 128, 128), 128)
                    lanes = slice(half * 128, (half + 1) * 128)
                    cell = result_ref[6:7, part]
                    cell_high = result_ref[7:8, part]
                    same_ref[step, :, lanes] = jnp.where(cell_col[...] == cell, 1.0, 0.0).astype(BF16)
                    after_ref[step, :, lanes] = jnp.where(high_col[...] == cell, 1.0, 0.0).astype(BF16)
                    before_ref[step, :, lanes] = jnp.where(cell_col[...] == cell_high, 1.0, 0.0).astype(BF16)
            left = left_ref[...]

            def product(table):
                out = jnp.dot(left, table, preferred_element_type=F32)
                return out[0:16] + out[16:32] + out[32:48]

            same = product(same_ref[step])
            after = product(after_ref[step])
            before = product(before_ref[step])
            share = pack_ref[3:4, at]
            total = (1.0 - share) * (same[0:8] + after[8:16]) + share * (same[8:16] + before[0:8])
            result_ref[0:6, at] = SPREAD_GAIN * total[0:6]
            return carry

        lax.fori_loop(0, steps, one, 0)

    prepare()
    apply(True)
    arm = pack_ref[4:7, :]
    weight = pack_ref[2:3, :]
    first = state_ref[0:3, :]
    second = first - result_ref[0:3, :]
    carried = result_ref[3:6, :]
    state_ref[0:3, :] = second
    state_ref[3:6, :] = carried
    prepare()
    apply(False)
    third = second - result_ref[0:3, :]
    later = carried - result_ref[3:6, :]
    heavy = arm * weight
    rows = []
    for vector in (arm, carried, later):
        for a in range(3):
            rows.append(heavy[a : a + 1] * vector)
    for vector in (first, second, third):
        rows.append(heavy[1:2] * vector[2:3] - heavy[2:3] * vector[1:2])
        rows.append(heavy[2:3] * vector[0:1] - heavy[0:1] * vector[2:3])
        rows.append(heavy[0:1] * vector[1:2] - heavy[1:2] * vector[0:1])
    rows.append(jnp.zeros((4, slots), F32))
    table = jnp.concatenate(rows, axis=0)
    sums_ref[...] = jnp.broadcast_to(jnp.sum(table, axis=1, keepdims=True), sums_ref.shape)
    linear_ref[0:3, :] = heavy
    linear_ref[3:6, :] = weight * (first + second + third)
    linear_ref[6:9, :] = weight * (carried + later)
    linear_ref[9:12, :] = weight * carried
    linear_ref[12:16, :] = jnp.zeros((4, slots), F32)


def total_kernel(x_count, y_count, part_ref, out_ref, near, mine, far, near_send, near_recv, far_send, far_recv):
    x = lax.axis_index("gx")
    y = lax.axis_index("gy")
    barrier = pltpu.get_barrier_semaphore()
    for step in range(1, y_count):
        pl.semaphore_signal(barrier, inc=1, device_id=(x, lax.rem(y + step, y_count)), device_id_type=MESH)
    for step in range(1, x_count):
        pl.semaphore_signal(barrier, inc=1, device_id=(lax.rem(x + step, x_count), y), device_id_type=MESH)
    pl.semaphore_wait(barrier, x_count + y_count - 2)

    def near_copy(step):
        return pltpu.make_async_remote_copy(
            src_ref=part_ref,
            dst_ref=near.at[step - 1],
            send_sem=near_send.at[step - 1],
            recv_sem=near_recv.at[step - 1],
            device_id=(x, lax.rem(y + step, y_count)),
            device_id_type=MESH,
        )

    def far_copy(step):
        return pltpu.make_async_remote_copy(
            src_ref=mine,
            dst_ref=far.at[step - 1],
            send_sem=far_send.at[step - 1],
            recv_sem=far_recv.at[step - 1],
            device_id=(lax.rem(x + step, x_count), y),
            device_id_type=MESH,
        )

    def ordered(own, slots, count, position):
        total = None
        for source in range(count):
            value = own
            for step in range(1, count):
                hit = lax.rem(position + count - step, count) == source
                value = jnp.where(hit, slots[step - 1], value)
            total = value if total is None else total + value
        return total

    for step in range(1, y_count):
        near_copy(step).start()
    for step in range(1, y_count):
        near_copy(step).wait()
    mine[...] = ordered(part_ref[...], near, y_count, y)
    for step in range(1, x_count):
        far_copy(step).start()
    for step in range(1, x_count):
        far_copy(step).wait()
    out_ref[...] = ordered(mine[...], far, x_count, x)


def cross(first, second):
    return [
        first[1] * second[2] - first[2] * second[1],
        first[2] * second[0] - first[0] * second[2],
        first[0] * second[1] - first[1] * second[0],
    ]


def spread_kernel(
    rows_y,
    spin_ref,
    sums_ref,
    linear_ref,
    pack_ref,
    velocity_ref,
    density_ref,
    pops_ref,
    moved_ref,
    spins_ref,
    x_up_ref,
    x_down_ref,
    y_up_ref,
    y_down_ref,
    corner_a,
    corner_b,
    corner_c,
    corner_d,
    table_ref,
    hi_ref,
    lo_ref,
    x_in,
    y_in,
    x_sem,
    y_sem,
):
    planes, depth = density_ref.shape
    rows_x = planes // rows_y
    copies = []
    for number, m in enumerate(PLUS_X + MINUS_X):
        layer = rows_x - 1 if m in PLUS_X else 0
        copies.append(pltpu.make_async_copy(pops_ref.at[m, layer], x_in.at[number], x_sem.at[number]))
    for number, m in enumerate(PLUS_Y + MINUS_Y):
        row = rows_y - 1 if m in PLUS_Y else 0
        copies.append(pltpu.make_async_copy(pops_ref.at[m, :, row], y_in.at[number], y_sem.at[number]))
    for copy in copies:
        copy.start()

    def number_at(index):
        return sums_ref[index : index + 1, 0:1]

    def turning(offset, spin):
        entry = [[number_at(offset + a * 3 + b) for b in range(3)] for a in range(3)]
        trace = entry[0][0] + entry[1][1] + entry[2][2]
        return [
            spin[b] * trace - (entry[0][b] * spin[0] + entry[1][b] * spin[1] + entry[2][b] * spin[2])
            for b in range(3)
        ]

    inertia = number_at(0) + number_at(4) + number_at(8)
    spin = [spin_ref[0:1, number : number + 1] for number in range(3)]
    spins = [spin]
    spins_ref[...] = jnp.zeros(spins_ref.shape, F32)
    for step in range(ITERS):
        own = turning(0, spins[step])
        torque = [number_at(27 + step * 3 + b) - own[b] for b in range(3)]
        if step >= 1:
            back = turning(9, spins[step - 1])
            torque = [torque[b] + back[b] for b in range(3)]
        if step >= 2:
            back = turning(18, spins[step - 2])
            torque = [torque[b] + back[b] for b in range(3)]
        spins.append([spins[step][b] + SPIN_GAIN * torque[b] / inertia for b in range(3)])
        for b in range(3):
            spins_ref[step : step + 1, b : b + 1] = spins[step + 1][b]
    whole = [spins[0][b] + spins[1][b] + spins[2][b] for b in range(3)]

    def linear(start):
        return [linear_ref[start + b : start + b + 1, :] for b in range(3)]

    lead = cross(whole, linear(0))
    fall = linear(3)
    zeroth = cross(spins[0], linear(6))
    once = cross(spins[1], linear(9))
    impulse = [SPREAD_GAIN * (lead[b] - fall[b] - zeroth[b] - once[b]) for b in range(3)]
    table_ref[...] = plane_table(planes, pack_ref[0:1, :])
    tap = depth_table(depth, pack_ref[1:2, :], pack_ref[3:4, :])
    for number in range(3):
        lanes = slice(number * depth, (number + 1) * depth)
        hi, lo = pieces_of(tap * impulse[number], 2)
        hi_ref[...] = hi
        lo_ref[...] = lo
        dims = (((1,), (1,)), ((), ()))
        added = lax.dot_general(table_ref[...], hi_ref[...], dims, preferred_element_type=F32)
        added = added + lax.dot_general(table_ref[...], lo_ref[...], dims, preferred_element_type=F32)
        moved_ref[:, lanes] = velocity_ref[:, lanes] + added

    for copy in copies:
        copy.wait()

    def face(at, members, incoming, first):
        velocity = [moved_ref[at, number * depth : (number + 1) * depth] for number in range(3)]
        common = common_of(velocity)
        density = density_ref[at, :]
        return [
            relax(m, incoming[first + index], density, velocity, common)
            for index, m in enumerate(members)
        ]

    corners = {7: corner_a, 8: corner_b, 9: corner_c, 10: corner_d}
    for members, out, layer, first in (
        (PLUS_X, x_up_ref, rows_x - 1, 0),
        (MINUS_X, x_down_ref, 0, len(PLUS_X)),
    ):
        found = face(pl.ds(layer * rows_y, rows_y), members, x_in, first)
        for index, m in enumerate(members):
            out[index] = found[index]
            if m in DIAGONAL:
                row = rows_y - 1 if VELOCITY_TABLE[m][1] == 1 else 0
                corners[m][...] = found[index][row : row + 1]
    for members, out, row, first in (
        (PLUS_Y, y_up_ref, rows_y - 1, 0),
        (MINUS_Y, y_down_ref, 0, len(PLUS_Y)),
    ):
        def strided(ref, lanes):
            return jnp.concatenate(
                [ref[x * rows_y + row : x * rows_y + row + 1, lanes] for x in range(rows_x)], axis=0
            )

        velocity = [strided(moved_ref, slice(n * depth, (n + 1) * depth)) for n in range(3)]
        density = strided(density_ref, slice(0, depth))
        common = common_of(velocity)
        for index, m in enumerate(members):
            out[index] = relax(m, y_in[first + index], density, velocity, common)


def roll(value, steps, axis):
    if steps == 0:
        return value
    return pltpu.roll(value, steps % value.shape[axis], axis)


def collide_kernel(layers, pops_ref, velocity_ref, density_ref, out_ref, stage, sems):
    layer = pl.program_id(0)
    slot = lax.rem(layer, 2)
    depth = density_ref.shape[1]

    def each(which, at, action):
        for m in range(Q):
            step = VELOCITY_TABLE[m][0]

            def go(m=m, step=step):
                copy = pltpu.make_async_copy(stage.at[at, m], out_ref.at[m, which + step], sems.at[at, m])
                copy.start() if action == "start" else copy.wait()

            if step == 0:
                go()
            elif step == 1:
                pl.when(which < layers - 1)(go)
            else:
                pl.when(which > 0)(go)

    @pl.when(layer >= 2)
    def _():
        each(layer - 2, slot, "wait")

    velocity = [velocity_ref[:, n * depth : (n + 1) * depth] for n in range(3)]
    density = density_ref[...]
    common = common_of(velocity)
    for m in range(Q):
        value = relax(m, pops_ref[m, 0], density, velocity, common)
        value = roll(roll(value, VELOCITY_TABLE[m][1], 0), VELOCITY_TABLE[m][2], 1)
        stage[slot, m] = value
    each(layer, slot, "start")

    @pl.when(layer == layers - 1)
    def _():
        each(layer - 1, 1 - slot, "wait")
        each(layer, slot, "wait")


def edge_kernel(whole_ref, x_low, x_high, y_low, y_high, ca, cb, cc, cd, out_ref, face, strip, face_sem, strip_sem):
    del whole_ref
    layers, rows_y = out_ref.shape[1], out_ref.shape[2]
    corners = {7: ca, 8: cb, 9: cc, 10: cd}
    copies = []
    number = 0
    for members, source, layer in ((PLUS_X, x_low, 0), (MINUS_X, x_high, layers - 1)):
        for index, m in enumerate(members):
            step_y, step_z = VELOCITY_TABLE[m][1], VELOCITY_TABLE[m][2]
            value = source[index]
            if step_y == 1:
                value = jnp.concatenate([corners[m][...], value[: rows_y - 1]], axis=0)
            elif step_y == -1:
                value = jnp.concatenate([value[1:], corners[m][...]], axis=0)
            face[number] = roll(value, step_z, 1)
            copies.append(pltpu.make_async_copy(face.at[number], out_ref.at[m, layer], face_sem.at[number]))
            number += 1
    number = 0
    for members, source, row in ((PLUS_Y, y_low, 0), (MINUS_Y, y_high, rows_y - 1)):
        for index, m in enumerate(members):
            step_x, step_z = VELOCITY_TABLE[m][0], VELOCITY_TABLE[m][2]
            strip[number] = roll(source[index], step_z, 1)
            count = layers - abs(step_x)
            source_at = 1 if step_x == -1 else 0
            target_at = 1 if step_x == 1 else 0
            copies.append(
                pltpu.make_async_copy(
                    strip.at[number, pl.ds(source_at, count)],
                    out_ref.at[m, pl.ds(target_at, count), row],
                    strip_sem.at[number],
                )
            )
            number += 1
    for copy in copies:
        copy.start()
    for copy in copies:
        copy.wait()


def shifted(value, steps_x, steps_y):
    count_x, count_y = lax.axis_size("gx"), lax.axis_size("gy")
    pairs = []
    for x in range(count_x):
        for y in range(count_y):
            target = ((x + steps_x) % count_x) * count_y + (y + steps_y) % count_y
            pairs.append((x * count_y + y, target))
    return lax.ppermute(value, ("gx", "gy"), pairs)


def local(
    populations, rotation_init, slot_cell, slot_count, marker_arm, marker_area, marker_fraction
):
    _, size_x, size_y, depth = populations.shape
    slots = marker_area.shape[2]
    planes = size_x * size_y
    shape = jax.ShapeDtypeStruct
    params = pltpu.CompilerParams(vmem_limit_bytes=VMEM_LIMIT)
    cell = slot_cell.reshape(3, slots)
    plane = (cell[0] - lax.axis_index("gx") * size_x) * size_y + cell[1] - lax.axis_index("gy") * size_y
    active = lax.broadcasted_iota(jnp.int32, (slots,), 0) < slot_count.reshape(())
    weight = jnp.where(active, marker_area.reshape(-1), 0.0)
    pack = jnp.concatenate(
        [
            plane.astype(F32)[None],
            cell[2].astype(F32)[None],
            weight[None],
            marker_fraction.reshape(1, slots),
            marker_arm.reshape(3, slots),
            jnp.zeros((1, slots), F32),
        ],
        axis=0,
    )
    density, velocity = pl.pallas_call(
        moments_kernel,
        grid=(size_x,),
        in_specs=[pl.BlockSpec((Q, 1, size_y, depth), lambda x: (0, x, 0, 0))],
        out_specs=[
            pl.BlockSpec((size_y, depth), lambda x: (x, 0)),
            pl.BlockSpec((size_y, 3 * depth), lambda x: (x, 0)),
        ],
        out_shape=[shape((planes, depth), F32), shape((planes, 3 * depth), F32)],
        name="moments",
    )(populations)
    table = VMEM((slots // 256, slots, 256), BF16)
    sums, linear = pl.pallas_call(
        gather_kernel,
        in_specs=[vmem()] * 2,
        out_specs=[vmem()] * 2,
        out_shape=[shape((40, 128), F32), shape((16, slots), F32)],
        scratch_shapes=[
            VMEM((3 * depth, planes), BF16),
            VMEM((3 * depth, planes), BF16),
            VMEM((8, slots), F32),
            VMEM((8, slots), F32),
            VMEM((slots, 128), F32),
            VMEM((slots, 128), F32),
            table,
            table,
            table,
            VMEM((48, slots), BF16),
        ],
        compiler_params=params,
        name="gather",
    )(velocity, pack)
    count_x, count_y = lax.axis_size("gx"), lax.axis_size("gy")
    dma = pltpu.SemaphoreType.DMA
    sums = pl.pallas_call(
        functools.partial(total_kernel, count_x, count_y),
        in_specs=[vmem()],
        out_specs=vmem(),
        out_shape=shape((40, 128), F32),
        scratch_shapes=[
            VMEM((count_y - 1, 40, 128), F32),
            VMEM((40, 128), F32),
            VMEM((count_x - 1, 40, 128), F32),
            dma((count_y - 1,)),
            dma((count_y - 1,)),
            dma((count_x - 1,)),
            dma((count_x - 1,)),
        ],
        compiler_params=pltpu.CompilerParams(collective_id=0, has_side_effects=True),
        name="total",
    )(sums)
    x_face = shape((len(PLUS_X), size_y, depth), F32)
    y_face = shape((len(PLUS_Y), size_x, depth), F32)
    corner = shape((1, depth), F32)
    moved, spins, x_up, x_down, y_up, y_down, c7, c8, c9, c10 = pl.pallas_call(
        functools.partial(spread_kernel, size_y),
        in_specs=[vmem()] * 6 + [pl.BlockSpec(memory_space=pl.ANY)],
        out_specs=[vmem()] * 10,
        out_shape=[
            shape((planes, 3 * depth), F32),
            shape((8, 128), F32),
            x_face,
            x_face,
            y_face,
            y_face,
            corner,
            corner,
            corner,
            corner,
        ],
        scratch_shapes=[
            VMEM((planes, slots), BF16),
            VMEM((depth, slots), BF16),
            VMEM((depth, slots), BF16),
            VMEM((2 * len(PLUS_X), size_y, depth), F32),
            VMEM((2 * len(PLUS_Y), size_x, depth), F32),
            dma((2 * len(PLUS_X),)),
            dma((2 * len(PLUS_Y),)),
        ],
        compiler_params=params,
        name="spread",
    )(rotation_init.reshape(1, 3), sums, linear, pack, velocity, density, populations)
    x_low = shifted(x_up, 1, 0)
    x_high = shifted(x_down, -1, 0)
    y_low = shifted(y_up, 0, 1)
    y_high = shifted(y_down, 0, -1)
    c7, c8 = shifted(c7, 1, 1), shifted(c8, -1, -1)
    c9, c10 = shifted(c9, 1, -1), shifted(c10, -1, 1)
    whole = pl.pallas_call(
        functools.partial(collide_kernel, size_x),
        grid=(size_x,),
        in_specs=[
            pl.BlockSpec((Q, 1, size_y, depth), lambda x: (0, x, 0, 0)),
            pl.BlockSpec((size_y, 3 * depth), lambda x: (x, 0)),
            pl.BlockSpec((size_y, depth), lambda x: (x, 0)),
        ],
        out_specs=pl.BlockSpec(memory_space=pl.ANY),
        out_shape=shape(populations.shape, F32),
        scratch_shapes=[VMEM((2, Q, size_y, depth), F32), dma((2, Q))],
        cost_estimate=pl.CostEstimate(flops=100_000_000, bytes_accessed=20_000_000, transcendentals=0),
        name="collide",
    )(populations, moved, density)
    whole = pl.pallas_call(
        edge_kernel,
        in_specs=[pl.BlockSpec(memory_space=pl.ANY)] + [vmem()] * 8,
        out_specs=pl.BlockSpec(memory_space=pl.ANY),
        out_shape=shape(populations.shape, F32),
        scratch_shapes=[
            VMEM((2 * len(PLUS_X), size_y, depth), F32),
            VMEM((2 * len(PLUS_Y), size_x, depth), F32),
            dma((2 * len(PLUS_X),)),
            dma((2 * len(PLUS_Y),)),
        ],
        input_output_aliases={0: 0},
        name="edges",
    )(whole, x_low, x_high, y_low, y_high, c7, c8, c9, c10)
    return whole, spins[:ITERS, :3]


def solution(mesh):
    return jax.shard_map(
        local,
        mesh=mesh,
        in_specs=(
            P(None, "gx", "gy", None),
            P(),
            P(None, "gx", "gy", None),
            P("gx", "gy"),
            P(None, "gx", "gy", None),
            P("gx", "gy", None),
            P("gx", "gy", None),
        ),
        out_specs=(P(None, "gx", "gy", None), P()),
        check_vma=False,
    )
```

profile of v0, /device:TPU:0, one launch (start us, length us, event | category | flops | bytes accessed | tf_op | source)
XLA Modules:
  0.0 102.0 jit_solution(17965195773692099468)
XLA Ops:
  0.6 0.0 copy-start.6
  0.6 0.0 copy-start.4
  0.7 0.0 copy-start.5
  1.3 0.8 copy.12
  2.1 7.6 %moments.1 = (f32[512,256]{1,0:T(8,128)}, f32[512,768]{1,0:T(8,128)}) custom-call(f32[19,8,64,256]{3,2,1,0:T(8,128)} %pops_ref.5), custom_call_target="tpu_custom_call" | custom-call | tf_op jit(solution)/shard_map/moments/pallas_call | solution.py:535
  9.7 0.0 copy-done.6
  9.7 0.0 copy-done.4
  9.7 0.0 copy-done.5
  9.7 0.7 concatenate.3.pack_ref
  10.4 21.9 %gather.1 = (f32[40,128]{1,0:T(8,128)}, f32[16,2048]{1,0:T(8,128)}) custom-call(f32[512,768]{1,0:T(8,128)} %get-tuple-element.16.velocity_ref, f32[8,2048]{1,0:T(8,128)} %concatenate.3.pack_ref), custom_call_target="tpu_custom_call" | custom-call | tf_op jit(solution)/shard_map/gather/pallas_call | solution.py:547
  32.3 14.7 %total.1.sums_ref = f32[40,128]{1,0:T(8,128)} custom-call(f32[40,128]{1,0:T(8,128)} %get-tuple-element.17.part_ref), custom_call_target="tpu_custom_call" | custom-call | tf_op jit(solution)/shard_map/total/pallas_call | solution.py:569
  47.0 7.6 %spread.1 = (f32[512,768]{1,0:T(8,128)}, f32[8,128]{1,0:T(8,128)}, f32[5,64,256]{2,1,0:T(8,128)}, f32[5,64,256]{2,1,0:T(8,128)}, f32[5,8,256]{2,1,0:T(8,128)}, /...) custom-call(f32[1,3]{1,0:T(1,128)} %bitcast.15, ...), custom_call_target="tpu_custom_call" | custom-call | tf_op jit(solution)/shard_map/spread/pallas_call | solution.py:589
  54.6 2.0 %collective-permute-start = (f32[5,64,256]{2,1,0:T(8,128)}, f32[5,64,256]{2,1,0:T(8,128)S(1)}, u32[]{:S(2)}, u32[]{:S(2)}) collective-permute-start(f32[5,64,256]{2,1,0:T(8,128)} %get-tuple-element.21), channel_id=1, source_target_pairs={{0,4},{1,5},{2,6},{3,7},{4,8},{5,9},{6,10},{7,11},{8,12},{9,13},{1... | collective-permute-start | bytes 983048 | tf_op jit(solution)/shard_map/ppermute | solution.py:509
  56.6 2.8 %collective-permute-start.1 = (f32[5,64,256]{2,1,0:T(8,128)}, f32[5,64,256]{2,1,0:T(8,128)S(1)}, u32[]{:S(2)}, u32[]{:S(2)}) collective-permute-start(f32[5,64,256]{2,1,0:T(8,128)} %get-tuple-element.22), channel_id=1, source_target_pairs={{0,28},{1,29},{2,30},{3,31},{4,0},{5,1},{6,2},{7,3},{8,4},{9,5},{1... | collective-permute-start | bytes 983048 | tf_op jit(solution)/shard_map/ppermute | solution.py:509
  59.4 0.0 collective-permute-start.2
  59.4 1.7 %collective-permute-start.3 = (f32[5,8,256]{2,1,0:T(8,128)}, f32[5,8,256]{2,1,0:T(8,128)S(1)}, u32[]{:S(2)}, u32[]{:S(2)}) collective-permute-start(f32[5,8,256]{2,1,0:T(8,128)} %get-tuple-element.24), channel_id=1, source_target_pairs={{0,3},{1,0},{2,1},{3,2},{4,7},{5,4},{6,5},{7,6},{8,11},{9,8},{10,9... | collective-permute-start | bytes 122888 | tf_op jit(solution)/shard_map/ppermute | solution.py:509
  61.1 0.0 collective-permute-start.4
  61.1 9.9 %collective-permute-done.4.ca = f32[1,256]{1,0:T(1,128)S(1)} collective-permute-done((f32[1,256]{1,0:T(1,128)}, f32[1,256]{1,0:T(1,128)S(1)}, u32[]{:S(2)}, u32[]{:S(2)}) %collective-permute-start.4) | collective-permute-done | bytes 1056 | tf_op jit(solution)/shard_map/ppermute | solution.py:509
  71.0 0.0 copy-start.7
  71.0 3.9 %collective-permute-start.5 = (f32[1,256]{1,0:T(1,128)}, f32[1,256]{1,0:T(1,128)S(1)}, u32[]{:S(2)}, u32[]{:S(2)}) collective-permute-start(f32[1,256]{1,0:T(1,128)} %get-tuple-element.26), channel_id=1, source_target_pairs={{0,31},{1,28},{2,29},{3,30},{4,3},{5,0},{6,1},{7,2},{8,7},{9,4},{1... | collective-permute-start | bytes 3080 | tf_op jit(solution)/shard_map/ppermute | solution.py:509
  75.0 1.5 %collective-permute-done.5.cb = f32[1,256]{1,0:T(1,128)S(1)} collective-permute-done((f32[1,256]{1,0:T(1,128)}, f32[1,256]{1,0:T(1,128)S(1)}, u32[]{:S(2)}, u32[]{:S(2)}) %collective-permute-start.5) | collective-permute-done | bytes 1056 | tf_op jit(solution)/shard_map/ppermute | solution.py:509
  76.5 0.0 copy-start.8
  76.5 1.6 %collective-permute-start.6 = (f32[1,256]{1,0:T(1,128)}, f32[1,256]{1,0:T(1,128)S(1)}, u32[]{:S(2)}, u32[]{:S(2)}) collective-permute-start(f32[1,256]{1,0:T(1,128)} %get-tuple-element.27), channel_id=1, source_target_pairs={{0,7},{1,4},{2,5},{3,6},{4,11},{5,8},{6,9},{7,10},{8,15},{9,12},{1... | collective-permute-start | bytes 3080 | tf_op jit(solution)/shard_map/ppermute | solution.py:509
  78.1 5.2 %collective-permute-done.6.cc = f32[1,256]{1,0:T(1,128)S(1)} collective-permute-done((f32[1,256]{1,0:T(1,128)}, f32[1,256]{1,0:T(1,128)S(1)}, u32[]{:S(2)}, u32[]{:S(2)}) %collective-permute-start.6) | collective-permute-done | bytes 1056 | tf_op jit(solution)/shard_map/ppermute | solution.py:509
  83.3 0.0 copy-start.9
  83.3 2.6 %collective-permute-start.7 = (f32[1,256]{1,0:T(1,128)}, f32[1,256]{1,0:T(1,128)S(1)}, u32[]{:S(2)}, u32[]{:S(2)}) collective-permute-start(f32[1,256]{1,0:T(1,128)} %get-tuple-element.28), channel_id=1, source_target_pairs={{0,29},{1,30},{2,31},{3,28},{4,1},{5,2},{6,3},{7,0},{8,5},{9,6},{1... | collective-permute-start | bytes 3080 | tf_op jit(solution)/shard_map/ppermute | solution.py:509
  85.9 0.0 copy-start.11
  85.9 11.6 %collide.1.whole_ref = f32[19,8,64,256]{3,2,1,0:T(8,128)} custom-call(f32[19,8,64,256]{3,2,1,0:T(8,128)} %pops_ref.5, f32[512,768]{1,0:T(8,128)} %get-tuple-element.20.velocity_ref, f32[512,256]{1,0:T(8,128)} %get-tuple-element.19.density_ref), custom_call_target="tpu_custom_call" | custom-call | flops 100000000 | bytes 20000000 | tf_op jit(solution)/shard_map/collide/pallas_call | solution.py:623
  97.6 0.0 copy-done.7
  97.6 0.0 copy-done.8
  97.6 0.0 copy-done.9
  97.6 0.0 copy-done.11
  97.6 0.6 slice.18
  98.2 0.0 collective-permute-done.7.cd
  98.2 0.0 copy-start.10
  98.2 0.0 collective-permute-done.2.y_low
  98.2 0.0 copy-start.2
  98.2 0.0 collective-permute-done.3.y_high
  98.2 0.0 copy-start.3
  98.2 0.0 collective-permute-done.x_low
  98.2 0.0 copy-start
  98.2 0.0 collective-permute-done.1.x_high
  98.3 0.5 copy-done.10
  98.8 0.0 copy-done.2
  98.8 0.0 copy-done.3
  98.8 0.1 copy-done
  99.0 0.7 copy-done.1
  99.7 2.3 %edges.1 = f32[19,8,64,256]{3,2,1,0:T(8,128)} custom-call(f32[19,8,64,256]{3,2,1,0:T(8,128)} %collide.1.whole_ref, f32[5,64,256]{2,1,0:T(8,128)} %copy-done, f32[5,64,256]{2,1,0:T(8,128)} %copy-done.1, f32[5,8,256]{2,1,0:T(8,128)} %copy-done.2, f32[5,8,256]{2,1,0:T(8,128)} %copy-done.3, f32[1,256]{1,0:T(1,128)} %copy-done.7, ...), custom_call_target="tpu_custom_call", output_to_operand_aliasing={{}: (0, {})} | custom-call | tf_op jit(solution)/shard_map/edges/pallas_call | solution.py:637
  (4 shorter events, 0.0 us)
Async XLA Ops:
  0.6 9.0 %copy-start.6 = (f32[1,1,2048]{2,1,0:T(1,128)S(1)}, f32[1,1,2048]{2,1,0:T(1,128)}, u32[]{:S(2)}) copy-start(f32[1,1,2048]{2,1,0:T(1,128)} %param.12) | copy-start | bytes 24580
  0.6 9.0 %copy-start.4 = (s32[3,1,1,2048]{3,2,1,0:T(1,128)S(1)}, s32[3,1,1,2048]{3,2,1,0:T(1,128)}, u32[]{:S(2)}) copy-start(s32[3,1,1,2048]{3,2,1,0:T(1,128)} %param.9) | copy-start | bytes 73732
  0.7 9.1 %copy-start.5 = (f32[1,1,2048]{2,1,0:T(1,128)S(1)}, f32[1,1,2048]{2,1,0:T(1,128)}, u32[]{:S(2)}) copy-start(f32[1,1,2048]{2,1,0:T(1,128)} %param.13) | copy-start | bytes 24580
  54.6 43.6 %collective-permute-start = (f32[5,64,256]{2,1,0:T(8,128)}, f32[5,64,256]{2,1,0:T(8,128)S(1)}, u32[]{:S(2)}, u32[]{:S(2)}) collective-permute-start(f32[5,64,256]{2,1,0:T(8,128)} %get-tuple-element.21), channel_id=1, source_target_pairs={{0,4},{1,5},{2,6},{3,7},{4,8},{5,9},{6,10},{7,11},{8,12},{9,13},{1... | collective-permute-start | bytes 983048 | tf_op jit(solution)/shard_map/ppermute | solution.py:509
  56.6 41.7 %collective-permute-start.1 = (f32[5,64,256]{2,1,0:T(8,128)}, f32[5,64,256]{2,1,0:T(8,128)S(1)}, u32[]{:S(2)}, u32[]{:S(2)}) collective-permute-start(f32[5,64,256]{2,1,0:T(8,128)} %get-tuple-element.22), channel_id=1, source_target_pairs={{0,28},{1,29},{2,30},{3,31},{4,0},{5,1},{6,2},{7,3},{8,4},{9,5},{1... | collective-permute-start | bytes 983048 | tf_op jit(solution)/shard_map/ppermute | solution.py:509
  59.4 38.8 %collective-permute-start.2 = (f32[5,8,256]{2,1,0:T(8,128)}, f32[5,8,256]{2,1,0:T(8,128)S(1)}, u32[]{:S(2)}, u32[]{:S(2)}) collective-permute-start(f32[5,8,256]{2,1,0:T(8,128)} %get-tuple-element.23), channel_id=1, source_target_pairs={{0,1},{1,2},{2,3},{3,0},{4,5},{5,6},{6,7},{7,4},{8,9},{9,10},{10,1... | collective-permute-start | bytes 122888 | tf_op jit(solution)/shard_map/ppermute | solution.py:509
  59.4 38.8 %collective-permute-start.3 = (f32[5,8,256]{2,1,0:T(8,128)}, f32[5,8,256]{2,1,0:T(8,128)S(1)}, u32[]{:S(2)}, u32[]{:S(2)}) collective-permute-start(f32[5,8,256]{2,1,0:T(8,128)} %get-tuple-element.24), channel_id=1, source_target_pairs={{0,3},{1,0},{2,1},{3,2},{4,7},{5,4},{6,5},{7,6},{8,11},{9,8},{10,9... | collective-permute-start | bytes 122888 | tf_op jit(solution)/shard_map/ppermute | solution.py:509
  61.1 9.9 %collective-permute-start.4 = (f32[1,256]{1,0:T(1,128)}, f32[1,256]{1,0:T(1,128)S(1)}, u32[]{:S(2)}, u32[]{:S(2)}) collective-permute-start(f32[1,256]{1,0:T(1,128)} %get-tuple-element.25), channel_id=1, source_target_pairs={{0,5},{1,6},{2,7},{3,4},{4,9},{5,10},{6,11},{7,8},{8,13},{9,14},{1... | collective-permute-start | bytes 3080 | tf_op jit(solution)/shard_map/ppermute | solution.py:509
  71.0 26.5 %copy-start.7 = (f32[1,256]{1,0:T(1,128)}, f32[1,256]{1,0:T(1,128)S(1)}, u32[]{:S(2)}) copy-start(f32[1,256]{1,0:T(1,128)S(1)} %collective-permute-done.4.ca) | copy-start | bytes 3076
  71.0 5.4 %collective-permute-start.5 = (f32[1,256]{1,0:T(1,128)}, f32[1,256]{1,0:T(1,128)S(1)}, u32[]{:S(2)}, u32[]{:S(2)}) collective-permute-start(f32[1,256]{1,0:T(1,128)} %get-tuple-element.26), channel_id=1, source_target_pairs={{0,31},{1,28},{2,29},{3,30},{4,3},{5,0},{6,1},{7,2},{8,7},{9,4},{1... | collective-permute-start | bytes 3080 | tf_op jit(solution)/shard_map/ppermute | solution.py:509
  76.5 21.1 %copy-start.8 = (f32[1,256]{1,0:T(1,128)}, f32[1,256]{1,0:T(1,128)S(1)}, u32[]{:S(2)}) copy-start(f32[1,256]{1,0:T(1,128)S(1)} %collective-permute-done.5.cb) | copy-start | bytes 3076
  76.5 6.8 %collective-permute-start.6 = (f32[1,256]{1,0:T(1,128)}, f32[1,256]{1,0:T(1,128)S(1)}, u32[]{:S(2)}, u32[]{:S(2)}) collective-permute-start(f32[1,256]{1,0:T(1,128)} %get-tuple-element.27), channel_id=1, source_target_pairs={{0,7},{1,4},{2,5},{3,6},{4,11},{5,8},{6,9},{7,10},{8,15},{9,12},{1... | collective-permute-start | bytes 3080 | tf_op jit(solution)/shard_map/ppermute | solution.py:509
  83.3 14.3 %copy-start.9 = (f32[1,256]{1,0:T(1,128)}, f32[1,256]{1,0:T(1,128)S(1)}, u32[]{:S(2)}) copy-start(f32[1,256]{1,0:T(1,128)S(1)} %collective-permute-done.6.cc) | copy-start | bytes 3076
  83.3 14.9 %collective-permute-start.7 = (f32[1,256]{1,0:T(1,128)}, f32[1,256]{1,0:T(1,128)S(1)}, u32[]{:S(2)}, u32[]{:S(2)}) collective-permute-start(f32[1,256]{1,0:T(1,128)} %get-tuple-element.28), channel_id=1, source_target_pairs={{0,29},{1,30},{2,31},{3,28},{4,1},{5,2},{6,3},{7,0},{8,5},{9,6},{1... | collective-permute-start | bytes 3080 | tf_op jit(solution)/shard_map/ppermute | solution.py:509
  85.9 11.7 %copy-start.11 = (f32[8,128]{1,0:T(8,128)S(1)}, f32[8,128]{1,0:T(8,128)}, u32[]{:S(2)}) copy-start(f32[8,128]{1,0:T(8,128)} %get-tuple-element.29) | copy-start | bytes 12292
  98.2 0.6 copy-start.10
  98.2 0.6 copy-start.2
  98.2 0.6 copy-start.3
  98.2 0.7 copy-start
  99.0 0.7 copy-start.1
where the time goes:
time: 103 us; the launch traced here: 102 us
  Pallas kernels  65.6 us (64%)
  waiting for transfers between devices  16.7 us (16%)
  starting transfers between devices  14.7 us (14%)
  local copies, waits for them, and re-layouts  3.5 us (3%)
  between operations  1.48 us (1%)
    pallas_call x1, Pallas kernels, local(): pl.pallas_call(gather_kernel, in_specs=[vmem()] * 2, out_specs=[vmem()] *...  21.9 us
    ppermute x8, waiting for transfers between devices, shifted(): return lax.ppermute(value, ('gx', 'gy'), pairs)  16.7 us
    pallas_call x1, Pallas kernels, local(): pl.pallas_call(functools.partial(total_kernel, count_x, count_y), in_spec...  14.7 us
    ppermute x8, starting transfers between devices, shifted(): return lax.ppermute(value, ('gx', 'gy'), pairs)  14.7 us
    pallas_call x1, Pallas kernels, local(): pl.pallas_call(functools.partial(collide_kernel, size_x), grid=(size_x,),...  11.6 us
    pallas_call x1, Pallas kernels, local(): pl.pallas_call(moments_kernel, grid=(size_x,), in_specs=[pl.BlockSpec((Q,...  7.56 us
    pallas_call x1, Pallas kernels, local(): pl.pallas_call(functools.partial(spread_kernel, size_y), in_specs=[vmem()...  7.56 us
    pallas_call x1, Pallas kernels, local(): pl.pallas_call(edge_kernel, in_specs=[pl.BlockSpec(memory_space=pl.ANY)]...  2.27 us
  transfers between devices with their start and end apart: 8, of which 3 were waited for; matrix products, arithmetic and copies ran while one was open for 1% of the time, Pallas kernels for 11%

commit v1 on v0

--- a/solution.py
+++ b/solution.py
@@ -70,23 +70,36 @@
     return 1.0 - 1.5 * squared
 
 
-def moments_kernel(pops_ref, density_ref, velocity_ref):
-    depth = pops_ref.shape[3]
-    values = [pops_ref[m, 0] for m in range(Q)]
-    density = values[0]
-    for m in range(1, Q):
-        density = density + values[m]
-    density_ref[...] = density
-    for number in range(3):
-        total = None
-        for m in range(Q):
-            direction = VELOCITY_TABLE[m][number]
-            if direction != 0:
-                if total is None:
-                    total = values[m]
-                else:
-                    total = total + values[m] if direction > 0 else total - values[m]
-        velocity_ref[:, number * depth : (number + 1) * depth] = total / density
+def moments_kernel(pops_ref, density_ref, velocity_ref, held, sems):
+    layers, size_y, depth = pops_ref.shape[1], pops_ref.shape[2], pops_ref.shape[3]
+
+    def incoming(layer):
+        return pltpu.make_async_copy(pops_ref.at[:, layer], held.at[layer], sems.at[layer])
+
+    for layer in range(layers):
+        incoming(layer).start()
+
+    def one(layer, carry):
+        incoming(layer).wait()
+        at = pl.ds(pl.multiple_of(layer * size_y, size_y), size_y)
+        values = [held[layer, m] for m in range(Q)]
+        density = values[0]
+        for m in range(1, Q):
+            density = density + values[m]
+        density_ref[at, :] = density
+        for number in range(3):
+            total = None
+            for m in range(Q):
+                direction = VELOCITY_TABLE[m][number]
+                if direction != 0:
+                    if total is None:
+                        total = values[m]
+                    else:
+                        total = total + values[m] if direction > 0 else total - values[m]
+            velocity_ref[at, number * depth : (number + 1) * depth] = total / density
+        return carry
+
+    lax.fori_loop(0, layers, one, 0)
 
 
 def pieces_of(value, count):
@@ -220,7 +233,9 @@
         rows.append(heavy[0:1] * vector[1:2] - heavy[1:2] * vector[0:1])
     rows.append(jnp.zeros((4, slots), F32))
     table = jnp.concatenate(rows, axis=0)
-    sums_ref[...] = jnp.broadcast_to(jnp.sum(table, axis=1, keepdims=True), sums_ref.shape)
+    column = jnp.broadcast_to(jnp.sum(table, axis=1, keepdims=True), (40, 128))
+    square = jnp.concatenate([column, jnp.zeros((88, 128), F32)], axis=0)
+    sums_ref[...] = jnp.transpose(square)[0:8]
     linear_ref[0:3, :] = heavy
     linear_ref[3:6, :] = weight * (first + second + third)
     linear_ref[6:9, :] = weight * (carried + later)
@@ -312,6 +327,7 @@
     lo_ref,
     x_in,
     y_in,
+    turned,
     x_sem,
     y_sem,
 ):
@@ -327,8 +343,10 @@
     for copy in copies:
         copy.start()
 
+    turned[...] = jnp.transpose(jnp.broadcast_to(sums_ref[0:1, :], (128, 128)))
+
     def number_at(index):
-        return sums_ref[index : index + 1, 0:1]
+        return turned[index : index + 1, 0:1]
 
     def turning(offset, spin):
         entry = [[number_at(offset + a * 3 + b) for b in range(3)] for a in range(3)]
@@ -421,43 +439,87 @@
     return pltpu.roll(value, steps % value.shape[axis], axis)
 
 
-def collide_kernel(layers, pops_ref, velocity_ref, density_ref, out_ref, stage, sems):
-    layer = pl.program_id(0)
-    slot = lax.rem(layer, 2)
-    depth = density_ref.shape[1]
-
-    def each(which, at, action):
+def collide_kernel(layers, pops_ref, velocity_ref, density_ref, out_ref, held, speed, mass, in_sems, sems):
+    size_y, depth = held.shape[2], held.shape[3]
+
+    def incoming(layer):
+        rows = pl.ds(pl.multiple_of(layer * size_y, size_y), size_y)
+        return [
+            pltpu.make_async_copy(pops_ref.at[:, layer], held.at[layer], in_sems.at[0, layer]),
+            pltpu.make_async_copy(velocity_ref.at[rows], speed.at[layer], in_sems.at[1, layer]),
+            pltpu.make_async_copy(density_ref.at[rows], mass.at[layer], in_sems.at[2, layer]),
+        ]
+
+    def outgoing(layer, action):
         for m in range(Q):
             step = VELOCITY_TABLE[m][0]
 
             def go(m=m, step=step):
-                copy = pltpu.make_async_copy(stage.at[at, m], out_ref.at[m, which + step], sems.at[at, m])
+                copy = pltpu.make_async_copy(held.at[layer, m], out_ref.at[m, layer + step], sems.at[layer, m])
                 copy.start() if action == "start" else copy.wait()
 
             if step == 0:
                 go()
             elif step == 1:
-                pl.when(which < layers - 1)(go)
+                pl.when(layer < layers - 1)(go)
             else:
-                pl.when(which > 0)(go)
-
-    @pl.when(layer >= 2)
-    def _():
-        each(layer - 2, slot, "wait")
-
-    velocity = [velocity_ref[:, n * depth : (n + 1) * depth] for n in range(3)]
-    density = density_ref[...]
-    common = common_of(velocity)
-    for m in range(Q):
-        value = relax(m, pops_ref[m, 0], density, velocity, common)
-        value = roll(roll(value, VELOCITY_TABLE[m][1], 0), VELOCITY_TABLE[m][2], 1)
-        stage[slot, m] = value
-    each(layer, slot, "start")
-
-    @pl.when(layer == layers - 1)
-    def _():
-        each(layer - 1, 1 - slot, "wait")
-        each(layer, slot, "wait")
+                pl.when(layer > 0)(go)
+
+    for layer in range(layers):
+        for copy in incoming(layer):
+            copy.start()
+
+    def one(layer, carry):
+        for copy in incoming(layer):
+            copy.wait()
+        velocity = [speed[layer, :, n * depth : (n + 1) * depth] for n in range(3)]
+        density = mass[layer]
+        common = common_of(velocity)
+        for m in range(Q):
+            value = relax(m, held[layer, m], density, velocity, common)
+            value = roll(roll(value, VELOCITY_TABLE[m][1], 0), VELOCITY_TABLE[m][2], 1)
+            held[layer, m] = value
+        outgoing(layer, "start")
+        return carry
+
+    lax.fori_loop(0, layers, one, 0)
+
+    def finish(layer, carry):
+        outgoing(layer, "wait")
+        return carry
+
+    lax.fori_loop(0, layers, finish, 0)
+
+
+def trade_kernel(x_count, y_count, *refs):
+    ways = ((0, 1), (0, -1), (1, 1), (-1, -1), (1, -1), (-1, 1))
+    count = len(ways)
+    sources, targets, slots = refs[:count], refs[count : 2 * count], refs[2 * count : 3 * count]
+    send_sem, recv_sem = refs[3 * count :]
+    x = lax.axis_index("gx")
+    y = lax.axis_index("gy")
+    others = [(lax.rem(x + dx + x_count, x_count), lax.rem(y + dy + y_count, y_count)) for dx, dy in ways]
+    barrier = pltpu.get_barrier_semaphore()
+    for other in others:
+        pl.semaphore_signal(barrier, inc=1, device_id=other, device_id_type=MESH)
+    pl.semaphore_wait(barrier, count)
+    copies = [
+        pltpu.make_async_remote_copy(
+            src_ref=sources[n],
+            dst_ref=slots[n],
+            send_sem=send_sem.at[n],
+            recv_sem=recv_sem.at[n],
+            device_id=others[n],
+            device_id_type=MESH,
+        )
+        for n in range(count)
+    ]
+    for copy in copies:
+        copy.start()
+    for copy in copies:
+        copy.wait()
+    for n in range(count):
+        targets[n][...] = slots[n][...]
 
 
 def edge_kernel(whole_ref, x_low, x_high, y_low, y_high, ca, cb, cc, cd, out_ref, face, strip, face_sem, strip_sem):
@@ -532,15 +594,14 @@
         ],
         axis=0,
     )
+    held = VMEM((size_x, Q, size_y, depth), F32)
     density, velocity = pl.pallas_call(
         moments_kernel,
-        grid=(size_x,),
-        in_specs=[pl.BlockSpec((Q, 1, size_y, depth), lambda x: (0, x, 0, 0))],
-        out_specs=[
-            pl.BlockSpec((size_y, depth), lambda x: (x, 0)),
-            pl.BlockSpec((size_y, 3 * depth), lambda x: (x, 0)),
-        ],
+        in_specs=[pl.BlockSpec(memory_space=pl.ANY)],
+        out_specs=[vmem(), vmem()],
         out_shape=[shape((planes, depth), F32), shape((planes, 3 * depth), F32)],
+        scratch_shapes=[held, pltpu.SemaphoreType.DMA((size_x,))],
+        compiler_params=params,
         name="moments",
     )(populations)
     table = VMEM((slots // 256, slots, 256), BF16)
@@ -548,7 +609,7 @@
         gather_kernel,
         in_specs=[vmem()] * 2,
         out_specs=[vmem()] * 2,
-        out_shape=[shape((40, 128), F32), shape((16, slots), F32)],
+        out_shape=[shape((8, 128), F32), shape((16, slots), F32)],
         scratch_shapes=[
             VMEM((3 * depth, planes), BF16),
             VMEM((3 * depth, planes), BF16),
@@ -570,11 +631,11 @@
         functools.partial(total_kernel, count_x, count_y),
         in_specs=[vmem()],
         out_specs=vmem(),
-        out_shape=shape((40, 128), F32),
+        out_shape=shape((8, 128), F32),
         scratch_shapes=[
-            VMEM((count_y - 1, 40, 128), F32),
-            VMEM((40, 128), F32),
-            VMEM((count_x - 1, 40, 128), F32),
+            VMEM((count_y - 1, 8, 128), F32),
+            VMEM((8, 128), F32),
+            VMEM((count_x - 1, 8, 128), F32),
             dma((count_y - 1,)),
             dma((count_y - 1,)),
             dma((count_x - 1,)),
@@ -608,6 +669,7 @@
             VMEM((depth, slots), BF16),
             VMEM((2 * len(PLUS_X), size_y, depth), F32),
             VMEM((2 * len(PLUS_Y), size_x, depth), F32),
+            VMEM((128, 128), F32),
             dma((2 * len(PLUS_X),)),
             dma((2 * len(PLUS_Y),)),
         ],
@@ -616,21 +678,30 @@
     )(rotation_init.reshape(1, 3), sums, linear, pack, velocity, density, populations)
     x_low = shifted(x_up, 1, 0)
     x_high = shifted(x_down, -1, 0)
-    y_low = shifted(y_up, 0, 1)
-    y_high = shifted(y_down, 0, -1)
-    c7, c8 = shifted(c7, 1, 1), shifted(c8, -1, -1)
-    c9, c10 = shifted(c9, 1, -1), shifted(c10, -1, 1)
+    small = [y_face, y_face, corner, corner, corner, corner]
+    y_low, y_high, c7, c8, c9, c10 = pl.pallas_call(
+        functools.partial(trade_kernel, count_x, count_y),
+        in_specs=[vmem()] * 6,
+        out_specs=[vmem()] * 6,
+        out_shape=small,
+        scratch_shapes=[VMEM(one.shape, F32) for one in small] + [dma((6,)), dma((6,))],
+        compiler_params=pltpu.CompilerParams(collective_id=1, has_side_effects=True),
+        cost_estimate=pl.CostEstimate(flops=20_000_000, bytes_accessed=1_000_000, transcendentals=0),
+        name="trade",
+    )(y_up, y_down, c7, c8, c9, c10)
     whole = pl.pallas_call(
         functools.partial(collide_kernel, size_x),
-        grid=(size_x,),
-        in_specs=[
-            pl.BlockSpec((Q, 1, size_y, depth), lambda x: (0, x, 0, 0)),
-            pl.BlockSpec((size_y, 3 * depth), lambda x: (x, 0)),
-            pl.BlockSpec((size_y, depth), lambda x: (x, 0)),
-        ],
+        in_specs=[pl.BlockSpec(memory_space=pl.ANY)] * 3,
         out_specs=pl.BlockSpec(memory_space=pl.ANY),
         out_shape=shape(populations.shape, F32),
-        scratch_shapes=[VMEM((2, Q, size_y, depth), F32), dma((2, Q))],
+        scratch_shapes=[
+            held,
+            VMEM((size_x, size_y, 3 * depth), F32),
+            VMEM((size_x, size_y, depth), F32),
+            dma((3, size_x)),
+            dma((size_x, Q)),
+        ],
+        compiler_params=params,
         cost_estimate=pl.CostEstimate(flops=100_000_000, bytes_accessed=20_000_000, transcendentals=0),
         name="collide",
     )(populations, moved, density)

time: 103 us -> 81.9 us (0.80)
  waiting for transfers between devices: 16.7 us -> 0.01 us
  starting transfers between devices: 14.7 us -> 4.78 us
  Pallas kernels: 65.6 us -> 70.5 us
    ppermute x8 -> x2, waiting for transfers between devices: 16.7 us -> 0.01 us  [shifted(): return lax.ppermute(value, ('gx', 'gy'), pairs)]
    ppermute x8 -> x2, starting transfers between devices: 14.7 us -> 4.78 us  [shifted(): return lax.ppermute(value, ('gx', 'gy'), pairs)]
    pallas_call x2 -> x3, Pallas kernels: 19.2 us -> 25.8 us  [the longest x1 10.9 us: local(): pl.pallas_call(functools.partial(trade_kernel, count_x, count_y), in_spec...]
    pallas_call x1, Pallas kernels: 14.7 us -> 12.9 us  [local(): pl.pallas_call(functools.partial(total_kernel, count_x, count_y), in_spec...]
    unnamed x25 -> x11, local copies, waits for them, and re-layouts: 2.22 us -> 1.58 us
  transfers between devices with their start and end apart: 8 -> 2, of which waited for: 3 -> 0; matrix products, arithmetic and copies ran while one was open for 1% -> 2% of each run, Pallas kernels for 11% -> 25%
where the time goes in v1:
time: 81.9 us; the launch traced here: 80.3 us
  Pallas kernels  70.5 us (86%)
  starting transfers between devices  4.78 us (6%)
  local copies, waits for them, and re-layouts  3.53 us (4%)
  between operations  1.45 us (2%)
    pallas_call x1, Pallas kernels, local(): pl.pallas_call(gather_kernel, in_specs=[vmem()] * 2, out_specs=[vmem()] *...  22 us
    pallas_call x1, Pallas kernels, local(): pl.pallas_call(functools.partial(total_kernel, count_x, count_y), in_spec...  12.9 us
    pallas_call x1, Pallas kernels, local(): pl.pallas_call(functools.partial(trade_kernel, count_x, count_y), in_spec...  10.9 us
    pallas_call x1, Pallas kernels, local(): pl.pallas_call(functools.partial(collide_kernel, size_x), in_specs=[pl.Bl...  9.52 us
    pallas_call x1, Pallas kernels, local(): pl.pallas_call(functools.partial(spread_kernel, size_y), in_specs=[vmem()...  7.57 us
    pallas_call x1, Pallas kernels, local(): pl.pallas_call(moments_kernel, in_specs=[pl.BlockSpec(memory_space=pl.ANY...  5.34 us
    ppermute x2, starting transfers between devices, shifted(): return lax.ppermute(value, ('gx', 'gy'), pairs)  4.78 us
    pallas_call x1, Pallas kernels, local(): pl.pallas_call(edge_kernel, in_specs=[pl.BlockSpec(memory_space=pl.ANY)]...  2.27 us
  transfers between devices with their start and end apart: 2, of which 0 were waited for; matrix products, arithmetic and copies ran while one was open for 2% of the time, Pallas kernels for 25%

profile of v1, /device:TPU:0, one launch (start us, length us, event | category | flops | bytes accessed | tf_op | source)
XLA Modules:
  0.0 80.3 jit_solution(2354489817599056117)
XLA Ops:
  0.6 0.0 copy-start.4
  0.6 0.0 copy-start.2
  0.7 0.0 copy-start.3
  1.3 0.8 copy.12
  2.1 5.3 %moments.1 = (f32[512,256]{1,0:T(8,128)}, f32[512,768]{1,0:T(8,128)}) custom-call(f32[19,8,64,256]{3,2,1,0:T(8,128)} %pops_ref.5), custom_call_target="tpu_custom_call" | custom-call | tf_op jit(solution)/shard_map/moments/pallas_call | solution.py:598
  7.4 0.0 copy-done.4
  7.5 0.0 copy-done.2
  7.5 0.0 copy-done.3
  7.5 0.7 concatenate.3.pack_ref
  8.2 22.0 %gather.1 = (f32[8,128]{1,0:T(8,128)}, f32[16,2048]{1,0:T(8,128)}) custom-call(f32[512,768]{1,0:T(8,128)} %get-tuple-element.22.velocity_ref, f32[8,2048]{1,0:T(8,128)} %concatenate.3.pack_ref), custom_call_target="tpu_custom_call" | custom-call | tf_op jit(solution)/shard_map/gather/pallas_call | solution.py:608
  30.2 12.9 %total.1.sums_ref = f32[8,128]{1,0:T(8,128)} custom-call(f32[8,128]{1,0:T(8,128)} %get-tuple-element.23.part_ref), custom_call_target="tpu_custom_call" | custom-call | tf_op jit(solution)/shard_map/total/pallas_call | solution.py:630
  43.1 7.6 %spread.1 = (f32[512,768]{1,0:T(8,128)}, f32[8,128]{1,0:T(8,128)}, f32[5,64,256]{2,1,0:T(8,128)}, f32[5,64,256]{2,1,0:T(8,128)}, f32[5,8,256]{2,1,0:T(8,128)}, /...) custom-call(f32[1,3]{1,0:T(1,128)} %bitcast.15, ...), custom_call_target="tpu_custom_call" | custom-call | tf_op jit(solution)/shard_map/spread/pallas_call | solution.py:650
  50.7 1.6 %collective-permute-start = (f32[5,64,256]{2,1,0:T(8,128)}, f32[5,64,256]{2,1,0:T(8,128)S(1)}, u32[]{:S(2)}, u32[]{:S(2)}) collective-permute-start(f32[5,64,256]{2,1,0:T(8,128)} %get-tuple-element.27), channel_id=1, source_target_pairs={{0,4},{1,5},{2,6},{3,7},{4,8},{5,9},{6,10},{7,11},{8,12},{9,13},{1... | collective-permute-start | bytes 983048 | tf_op jit(solution)/shard_map/ppermute | solution.py:571
  52.3 3.2 %collective-permute-start.1 = (f32[5,64,256]{2,1,0:T(8,128)}, f32[5,64,256]{2,1,0:T(8,128)S(1)}, u32[]{:S(2)}, u32[]{:S(2)}) collective-permute-start(f32[5,64,256]{2,1,0:T(8,128)} %get-tuple-element.28), channel_id=1, source_target_pairs={{0,28},{1,29},{2,30},{3,31},{4,0},{5,1},{6,2},{7,3},{8,4},{9,5},{1... | collective-permute-start | bytes 983048 | tf_op jit(solution)/shard_map/ppermute | solution.py:571
  55.5 1.2 %slice.18 = f32[3,3]{1,0:T(4,128)} slice(f32[8,128]{1,0:T(8,128)} %get-tuple-element.41), slice={[0:3], [0:3]} | slice | bytes 72 | tf_op jit(solution)/shard_map/slice | solution.py:722
  56.7 10.9 %trade.1 = (f32[5,8,256]{2,1,0:T(8,128)}, f32[5,8,256]{2,1,0:T(8,128)}, f32[1,256]{1,0:T(1,128)}, f32[1,256]{1,0:T(1,128)}, f32[1,256]{1,0:T(1,128)}, /*index=5*/f32[1,256]{1,0:T(1,128)}) custom-call(f32[5,8,256]{2,1,0:T(8,128)} %get-tuple-element.29.refs_0_, f32[5,8,256]{2,1,0:T(8,128)} %get-tuple-element.30.refs_1_, f32[1,256]{1,0:T(1,128)} %get-tuple-element.31.refs_2_, ...), custom_call_target="tpu_custom_call" | custom-call | flops 20000000 | bytes 1000000 | tf_op jit(solution)/shard_map/trade/pallas_call | solution.py:682
  67.7 9.5 %collide.1.whole_ref = f32[19,8,64,256]{3,2,1,0:T(8,128)} custom-call(f32[19,8,64,256]{3,2,1,0:T(8,128)} %pops_ref.5, f32[512,768]{1,0:T(8,128)} %get-tuple-element.26.velocity_ref, f32[512,256]{1,0:T(8,128)} %get-tuple-element.25.density_ref), custom_call_target="tpu_custom_call" | custom-call | flops 100000000 | bytes 20000000 | tf_op jit(solution)/shard_map/collide/pallas_call | solution.py:692
  77.2 0.0 collective-permute-done.x_low
  77.2 0.0 copy-start
  77.2 0.0 collective-permute-done.1.x_high
  77.2 0.0 copy-start.1
  77.2 0.7 copy-done
  77.9 0.1 copy-done.1
  78.0 2.3 %edges.1 = f32[19,8,64,256]{3,2,1,0:T(8,128)} custom-call(f32[19,8,64,256]{3,2,1,0:T(8,128)} %collide.1.whole_ref, f32[5,64,256]{2,1,0:T(8,128)} %copy-done, f32[5,64,256]{2,1,0:T(8,128)} %copy-done.1, f32[5,8,256]{2,1,0:T(8,128)} %get-tuple-element.35.y_low, f32[5,8,256]{2,1,0:T(8,128)} %get-tuple-element.36.y_high, ...), custom_call_target="tpu_custom_call", output_to_operand_aliasing={{}: (0, {})} | custom-call | tf_op jit(solution)/shard_map/edges/pallas_call | solution.py:708
  (3 shorter events, 0.0 us)
Async XLA Ops:
  0.6 6.8 %copy-start.4 = (f32[1,1,2048]{2,1,0:T(1,128)S(1)}, f32[1,1,2048]{2,1,0:T(1,128)}, u32[]{:S(2)}) copy-start(f32[1,1,2048]{2,1,0:T(1,128)} %param.12) | copy-start | bytes 24580
  0.6 6.8 %copy-start.2 = (s32[3,1,1,2048]{3,2,1,0:T(1,128)S(1)}, s32[3,1,1,2048]{3,2,1,0:T(1,128)}, u32[]{:S(2)}) copy-start(s32[3,1,1,2048]{3,2,1,0:T(1,128)} %param.9) | copy-start | bytes 73732
  0.7 6.9 %copy-start.3 = (f32[1,1,2048]{2,1,0:T(1,128)S(1)}, f32[1,1,2048]{2,1,0:T(1,128)}, u32[]{:S(2)}) copy-start(f32[1,1,2048]{2,1,0:T(1,128)} %param.13) | copy-start | bytes 24580
  50.7 26.5 %collective-permute-start = (f32[5,64,256]{2,1,0:T(8,128)}, f32[5,64,256]{2,1,0:T(8,128)S(1)}, u32[]{:S(2)}, u32[]{:S(2)}) collective-permute-start(f32[5,64,256]{2,1,0:T(8,128)} %get-tuple-element.27), channel_id=1, source_target_pairs={{0,4},{1,5},{2,6},{3,7},{4,8},{5,9},{6,10},{7,11},{8,12},{9,13},{1... | collective-permute-start | bytes 983048 | tf_op jit(solution)/shard_map/ppermute | solution.py:571
  52.3 24.9 %collective-permute-start.1 = (f32[5,64,256]{2,1,0:T(8,128)}, f32[5,64,256]{2,1,0:T(8,128)S(1)}, u32[]{:S(2)}, u32[]{:S(2)}) collective-permute-start(f32[5,64,256]{2,1,0:T(8,128)} %get-tuple-element.28), channel_id=1, source_target_pairs={{0,28},{1,29},{2,30},{3,31},{4,0},{5,1},{6,2},{7,3},{8,4},{9,5},{1... | collective-permute-start | bytes 983048 | tf_op jit(solution)/shard_map/ppermute | solution.py:571
  77.2 0.7 copy-start
  77.2 0.8 %copy-start.1 = (f32[5,64,256]{2,1,0:T(8,128)}, f32[5,64,256]{2,1,0:T(8,128)S(1)}, u32[]{:S(2)}) copy-start(f32[5,64,256]{2,1,0:T(8,128)S(1)} %collective-permute-done.1.x_high) | copy-start | bytes 983044

commit v2 on v1

--- a/solution.py
+++ b/solution.py
@@ -146,7 +146,7 @@
     hi, lo = pieces_of(turned, 2)
     turned_hi[...] = hi
     turned_lo[...] = lo
-    chunk = 256
+    chunk = 512
     steps = slots // chunk
 
     def gather(step, carry):
@@ -387,12 +387,12 @@
     for number in range(3):
         lanes = slice(number * depth, (number + 1) * depth)
         hi, lo = pieces_of(tap * impulse[number], 2)
-        hi_ref[...] = hi
-        lo_ref[...] = lo
-        dims = (((1,), (1,)), ((), ()))
-        added = lax.dot_general(table_ref[...], hi_ref[...], dims, preferred_element_type=F32)
-        added = added + lax.dot_general(table_ref[...], lo_ref[...], dims, preferred_element_type=F32)
-        moved_ref[:, lanes] = velocity_ref[:, lanes] + added
+        hi_ref[lanes, :] = hi
+        lo_ref[lanes, :] = lo
+    dims = (((1,), (1,)), ((), ()))
+    added = lax.dot_general(table_ref[...], hi_ref[...], dims, preferred_element_type=F32)
+    added = added + lax.dot_general(table_ref[...], lo_ref[...], dims, preferred_element_type=F32)
+    moved_ref[...] = velocity_ref[...] + added
 
     for copy in copies:
         copy.wait()
@@ -494,8 +494,9 @@
 def trade_kernel(x_count, y_count, *refs):
     ways = ((0, 1), (0, -1), (1, 1), (-1, -1), (1, -1), (-1, 1))
     count = len(ways)
-    sources, targets, slots = refs[:count], refs[count : 2 * count], refs[2 * count : 3 * count]
-    send_sem, recv_sem = refs[3 * count :]
+    sources = refs[:count]
+    targets, slots = refs[count + 1 : 2 * count + 1], refs[2 * count + 1 : 3 * count + 1]
+    send_sem, recv_sem = refs[3 * count + 1 :]
     x = lax.axis_index("gx")
     y = lax.axis_index("gy")
     others = [(lax.rem(x + dx + x_count, x_count), lax.rem(y + dy + y_count, y_count)) for dx, dy in ways]
@@ -604,7 +605,7 @@
         compiler_params=params,
         name="moments",
     )(populations)
-    table = VMEM((slots // 256, slots, 256), BF16)
+    table = VMEM((slots // 512, slots, 512), BF16)
     sums, linear = pl.pallas_call(
         gather_kernel,
         in_specs=[vmem()] * 2,
@@ -665,8 +666,8 @@
         ],
         scratch_shapes=[
             VMEM((planes, slots), BF16),
-            VMEM((depth, slots), BF16),
-            VMEM((depth, slots), BF16),
+            VMEM((3 * depth, slots), BF16),
+            VMEM((3 * depth, slots), BF16),
             VMEM((2 * len(PLUS_X), size_y, depth), F32),
             VMEM((2 * len(PLUS_Y), size_x, depth), F32),
             VMEM((128, 128), F32),
@@ -678,17 +679,6 @@
     )(rotation_init.reshape(1, 3), sums, linear, pack, velocity, density, populations)
     x_low = shifted(x_up, 1, 0)
     x_high = shifted(x_down, -1, 0)
-    small = [y_face, y_face, corner, corner, corner, corner]
-    y_low, y_high, c7, c8, c9, c10 = pl.pallas_call(
-        functools.partial(trade_kernel, count_x, count_y),
-        in_specs=[vmem()] * 6,
-        out_specs=[vmem()] * 6,
-        out_shape=small,
-        scratch_shapes=[VMEM(one.shape, F32) for one in small] + [dma((6,)), dma((6,))],
-        compiler_params=pltpu.CompilerParams(collective_id=1, has_side_effects=True),
-        cost_estimate=pl.CostEstimate(flops=20_000_000, bytes_accessed=1_000_000, transcendentals=0),
-        name="trade",
-    )(y_up, y_down, c7, c8, c9, c10)
     whole = pl.pallas_call(
         functools.partial(collide_kernel, size_x),
         in_specs=[pl.BlockSpec(memory_space=pl.ANY)] * 3,
@@ -705,6 +695,17 @@
         cost_estimate=pl.CostEstimate(flops=100_000_000, bytes_accessed=20_000_000, transcendentals=0),
         name="collide",
     )(populations, moved, density)
+    small = [y_face, y_face, corner, corner, corner, corner]
+    y_low, y_high, c7, c8, c9, c10 = pl.pallas_call(
+        functools.partial(trade_kernel, count_x, count_y),
+        in_specs=[vmem()] * 6 + [pl.BlockSpec(memory_space=pl.ANY)],
+        out_specs=[vmem()] * 6,
+        out_shape=small,
+        scratch_shapes=[VMEM(one.shape, F32) for one in small] + [dma((6,)), dma((6,))],
+        compiler_params=pltpu.CompilerParams(collective_id=1, has_side_effects=True),
+        cost_estimate=pl.CostEstimate(flops=20_000_000, bytes_accessed=1_000_000, transcendentals=0),
+        name="trade",
+    )(y_up, y_down, c7, c8, c9, c10, whole)
     whole = pl.pallas_call(
         edge_kernel,
         in_specs=[pl.BlockSpec(memory_space=pl.ANY)] + [vmem()] * 8,

time: 81.9 us -> 76.3 us (0.932); the launches traced: 80.3 us -> 75.9 us
  Pallas kernels: 70.5 us -> 66.1 us
    pallas_call x1, Pallas kernels: 10.9 us -> 8.21 us  [local(): pl.pallas_call(functools.partial(trade_kernel, count_x, count_y), in_spec...]
    pallas_call x1, Pallas kernels: 22 us -> 20.1 us  [local(): pl.pallas_call(gather_kernel, in_specs=[vmem()] * 2, out_specs=[vmem()] *...]
  transfers between devices with their start and end apart: 2 -> 2, of which waited for: 0 -> 0; matrix products, arithmetic and copies ran while one was open for 2% -> 2% of each run, Pallas kernels for 25% -> 23%
where the time goes in v2:
time: 76.3 us; the launch traced here: 75.9 us
  Pallas kernels  66.1 us (87%)
  starting transfers between devices  4.78 us (6%)
  local copies, waits for them, and re-layouts  3.53 us (5%)
  between operations  1.45 us (2%)
    pallas_call x1, Pallas kernels, local(): pl.pallas_call(gather_kernel, in_specs=[vmem()] * 2, out_specs=[vmem()] *...  20.1 us
    pallas_call x1, Pallas kernels, local(): pl.pallas_call(functools.partial(total_kernel, count_x, count_y), in_spec...  12.9 us
    pallas_call x1, Pallas kernels, local(): pl.pallas_call(functools.partial(collide_kernel, size_x), in_specs=[pl.Bl...  9.51 us
    pallas_call x1, Pallas kernels, local(): pl.pallas_call(functools.partial(trade_kernel, count_x, count_y), in_spec...  8.21 us
    pallas_call x1, Pallas kernels, local(): pl.pallas_call(functools.partial(spread_kernel, size_y), in_specs=[vmem()...  7.75 us
    pallas_call x1, Pallas kernels, local(): pl.pallas_call(moments_kernel, in_specs=[pl.BlockSpec(memory_space=pl.ANY...  5.34 us
    ppermute x2, starting transfers between devices, shifted(): return lax.ppermute(value, ('gx', 'gy'), pairs)  4.78 us
    pallas_call x1, Pallas kernels, local(): pl.pallas_call(edge_kernel, in_specs=[pl.BlockSpec(memory_space=pl.ANY)]...  2.27 us
  transfers between devices with their start and end apart: 2, of which 0 were waited for; matrix products, arithmetic and copies ran while one was open for 2% of the time, Pallas kernels for 23%

profile of v2, /device:TPU:0, one launch (start us, length us, event | category | flops | bytes accessed | tf_op | source)
XLA Modules:
  0.0 75.9 jit_solution(17276196796121447372)
XLA Ops:
  0.6 0.0 copy-start.4
  0.6 0.0 copy-start.2
  0.7 0.0 copy-start.3
  1.3 0.8 copy.12
  2.1 5.3 %moments.1 = (f32[512,256]{1,0:T(8,128)}, f32[512,768]{1,0:T(8,128)}) custom-call(f32[19,8,64,256]{3,2,1,0:T(8,128)} %pops_ref.5), custom_call_target="tpu_custom_call" | custom-call | tf_op jit(solution)/shard_map/moments/pallas_call | solution.py:599
  7.4 0.0 copy-done.4
  7.5 0.0 copy-done.2
  7.5 0.0 copy-done.3
  7.5 0.7 concatenate.3.pack_ref
  8.2 20.1 %gather.1 = (f32[8,128]{1,0:T(8,128)}, f32[16,2048]{1,0:T(8,128)}) custom-call(f32[512,768]{1,0:T(8,128)} %get-tuple-element.22.velocity_ref, f32[8,2048]{1,0:T(8,128)} %concatenate.3.pack_ref), custom_call_target="tpu_custom_call" | custom-call | tf_op jit(solution)/shard_map/gather/pallas_call | solution.py:609
  28.3 12.9 %total.1.sums_ref = f32[8,128]{1,0:T(8,128)} custom-call(f32[8,128]{1,0:T(8,128)} %get-tuple-element.23.part_ref), custom_call_target="tpu_custom_call" | custom-call | tf_op jit(solution)/shard_map/total/pallas_call | solution.py:631
  41.3 7.7 %spread.1 = (f32[512,768]{1,0:T(8,128)}, f32[8,128]{1,0:T(8,128)}, f32[5,64,256]{2,1,0:T(8,128)}, f32[5,64,256]{2,1,0:T(8,128)}, f32[5,8,256]{2,1,0:T(8,128)}, /...) custom-call(f32[1,3]{1,0:T(1,128)} %bitcast.15, ...), custom_call_target="tpu_custom_call" | custom-call | tf_op jit(solution)/shard_map/spread/pallas_call | solution.py:651
  49.0 1.6 %collective-permute-start = (f32[5,64,256]{2,1,0:T(8,128)}, f32[5,64,256]{2,1,0:T(8,128)S(1)}, u32[]{:S(2)}, u32[]{:S(2)}) collective-permute-start(f32[5,64,256]{2,1,0:T(8,128)} %get-tuple-element.27), channel_id=1, source_target_pairs={{0,4},{1,5},{2,6},{3,7},{4,8},{5,9},{6,10},{7,11},{8,12},{9,13},{1... | collective-permute-start | bytes 983048 | tf_op jit(solution)/shard_map/ppermute | solution.py:572
  50.6 3.2 %collective-permute-start.1 = (f32[5,64,256]{2,1,0:T(8,128)}, f32[5,64,256]{2,1,0:T(8,128)S(1)}, u32[]{:S(2)}, u32[]{:S(2)}) collective-permute-start(f32[5,64,256]{2,1,0:T(8,128)} %get-tuple-element.28), channel_id=1, source_target_pairs={{0,28},{1,29},{2,30},{3,31},{4,0},{5,1},{6,2},{7,3},{8,4},{9,5},{1... | collective-permute-start | bytes 983048 | tf_op jit(solution)/shard_map/ppermute | solution.py:572
  53.8 1.2 %slice.18 = f32[3,3]{1,0:T(4,128)} slice(f32[8,128]{1,0:T(8,128)} %get-tuple-element.41), slice={[0:3], [0:3]} | slice | bytes 72 | tf_op jit(solution)/shard_map/slice | solution.py:723
  55.0 9.5 %collide.1.refs_6_.whole_ref = f32[19,8,64,256]{3,2,1,0:T(8,128)} custom-call(f32[19,8,64,256]{3,2,1,0:T(8,128)} %pops_ref.5, f32[512,768]{1,0:T(8,128)} %get-tuple-element.26.velocity_ref, f32[512,256]{1,0:T(8,128)} %get-tuple-element.25.density_ref), custom_call_target="tpu_custom_call" | custom-call | flops 100000000 | bytes 20000000 | tf_op jit(solution)/shard_map/collide/pallas_call | solution.py:682
  64.6 8.2 %trade.1 = (f32[5,8,256]{2,1,0:T(8,128)}, f32[5,8,256]{2,1,0:T(8,128)}, f32[1,256]{1,0:T(1,128)}, f32[1,256]{1,0:T(1,128)}, f32[1,256]{1,0:T(1,128)}, /*index=5*/f32[1,256]{1,0:T(1,128)}) custom-call(f32[5,8,256]{2,1,0:T(8,128)} %get-tuple-element.29.refs_0_, f32[5,8,256]{2,1,0:T(8,128)} %get-tuple-element.30.refs_1_, f32[1,256]{1,0:T(1,128)} %get-tuple-element.31.refs_2_, ...), custom_call_target="tpu_custom_call" | custom-call | flops 20000000 | bytes 1000000 | tf_op jit(solution)/shard_map/trade/pallas_call | solution.py:699
  72.8 0.0 collective-permute-done.x_low
  72.8 0.0 copy-start
  72.8 0.0 collective-permute-done.1.x_high
  72.8 0.0 copy-start.1
  72.8 0.7 copy-done
  73.5 0.1 copy-done.1
  73.6 2.3 %edges.1 = f32[19,8,64,256]{3,2,1,0:T(8,128)} custom-call(f32[19,8,64,256]{3,2,1,0:T(8,128)} %collide.1.refs_6_.whole_ref, f32[5,64,256]{2,1,0:T(8,128)} %copy-done, f32[5,64,256]{2,1,0:T(8,128)} %copy-done.1, f32[5,8,256]{2,1,0:T(8,128)} %get-tuple-element.35.y_low, f32[5,8,256]{2,1,0:T(8,128)} %get-tuple-element.36.y_high, ...), custom_call_target="tpu_custom_call", output_to_operand_aliasing={{}: (0, {})} | custom-call | tf_op jit(solution)/shard_map/edges/pallas_call | solution.py:709
  (3 shorter events, 0.0 us)
Async XLA Ops:
  0.6 6.8 %copy-start.4 = (f32[1,1,2048]{2,1,0:T(1,128)S(1)}, f32[1,1,2048]{2,1,0:T(1,128)}, u32[]{:S(2)}) copy-start(f32[1,1,2048]{2,1,0:T(1,128)} %param.12) | copy-start | bytes 24580
  0.6 6.8 %copy-start.2 = (s32[3,1,1,2048]{3,2,1,0:T(1,128)S(1)}, s32[3,1,1,2048]{3,2,1,0:T(1,128)}, u32[]{:S(2)}) copy-start(s32[3,1,1,2048]{3,2,1,0:T(1,128)} %param.9) | copy-start | bytes 73732
  0.7 6.9 %copy-start.3 = (f32[1,1,2048]{2,1,0:T(1,128)S(1)}, f32[1,1,2048]{2,1,0:T(1,128)}, u32[]{:S(2)}) copy-start(f32[1,1,2048]{2,1,0:T(1,128)} %param.13) | copy-start | bytes 24580
  49.0 23.8 %collective-permute-start = (f32[5,64,256]{2,1,0:T(8,128)}, f32[5,64,256]{2,1,0:T(8,128)S(1)}, u32[]{:S(2)}, u32[]{:S(2)}) collective-permute-start(f32[5,64,256]{2,1,0:T(8,128)} %get-tuple-element.27), channel_id=1, source_target_pairs={{0,4},{1,5},{2,6},{3,7},{4,8},{5,9},{6,10},{7,11},{8,12},{9,13},{1... | collective-permute-start | bytes 983048 | tf_op jit(solution)/shard_map/ppermute | solution.py:572
  50.6 22.2 %collective-permute-start.1 = (f32[5,64,256]{2,1,0:T(8,128)}, f32[5,64,256]{2,1,0:T(8,128)S(1)}, u32[]{:S(2)}, u32[]{:S(2)}) collective-permute-start(f32[5,64,256]{2,1,0:T(8,128)} %get-tuple-element.28), channel_id=1, source_target_pairs={{0,28},{1,29},{2,30},{3,31},{4,0},{5,1},{6,2},{7,3},{8,4},{9,5},{1... | collective-permute-start | bytes 983048 | tf_op jit(solution)/shard_map/ppermute | solution.py:572
  72.8 0.7 copy-start
  72.8 0.8 %copy-start.1 = (f32[5,64,256]{2,1,0:T(8,128)}, f32[5,64,256]{2,1,0:T(8,128)S(1)}, u32[]{:S(2)}) copy-start(f32[5,64,256]{2,1,0:T(8,128)S(1)} %collective-permute-done.1.x_high) | copy-start | bytes 983044

commit v3 on v2

--- a/solution.py
+++ b/solution.py
@@ -359,7 +359,6 @@
     inertia = number_at(0) + number_at(4) + number_at(8)
     spin = [spin_ref[0:1, number : number + 1] for number in range(3)]
     spins = [spin]
-    spins_ref[...] = jnp.zeros(spins_ref.shape, F32)
     for step in range(ITERS):
         own = turning(0, spins[step])
         torque = [number_at(27 + step * 3 + b) - own[b] for b in range(3)]
@@ -654,7 +653,7 @@
         out_specs=[vmem()] * 10,
         out_shape=[
             shape((planes, 3 * depth), F32),
-            shape((8, 128), F32),
+            shape((ITERS, 3), F32),
             x_face,
             x_face,
             y_face,
@@ -720,7 +719,7 @@
         input_output_aliases={0: 0},
         name="edges",
     )(whole, x_low, x_high, y_low, y_high, c7, c8, c9, c10)
-    return whole, spins[:ITERS, :3]
+    return whole, spins
 
 
 def solution(mesh):

time: 76.3 us -> 75 us (0.983)
  local copies, waits for them, and re-layouts: 3.53 us -> 2.28 us
    slice x1 -> x0, local copies, waits for them, and re-layouts: 1.25 us -> none  [local(): return (whole, spins[:ITERS, :3])]
  transfers between devices with their start and end apart: 2 -> 2, of which waited for: 0 -> 0; matrix products, arithmetic and copies ran while one was open for 2% -> 0% of each run, Pallas kernels for 23% -> 24%
where the time goes in v3:
time: 75 us; the launch traced here: 74.6 us
  Pallas kernels  66.1 us (88%)
  starting transfers between devices  4.78 us (6%)
  local copies, waits for them, and re-layouts  2.28 us (3%)
  between operations  1.45 us (2%)
    pallas_call x1, Pallas kernels, local(): pl.pallas_call(gather_kernel, in_specs=[vmem()] * 2, out_specs=[vmem()] *...  20.1 us
    pallas_call x1, Pallas kernels, local(): pl.pallas_call(functools.partial(total_kernel, count_x, count_y), in_spec...  12.9 us
    pallas_call x1, Pallas kernels, local(): pl.pallas_call(functools.partial(collide_kernel, size_x), in_specs=[pl.Bl...  9.51 us
    pallas_call x1, Pallas kernels, local(): pl.pallas_call(functools.partial(trade_kernel, count_x, count_y), in_spec...  8.21 us
    pallas_call x1, Pallas kernels, local(): pl.pallas_call(functools.partial(spread_kernel, size_y), in_specs=[vmem()...  7.73 us
    pallas_call x1, Pallas kernels, local(): pl.pallas_call(moments_kernel, in_specs=[pl.BlockSpec(memory_space=pl.ANY...  5.34 us
    ppermute x2, starting transfers between devices, shifted(): return lax.ppermute(value, ('gx', 'gy'), pairs)  4.78 us
    pallas_call x1, Pallas kernels, local(): pl.pallas_call(edge_kernel, in_specs=[pl.BlockSpec(memory_space=pl.ANY)]...  2.27 us
  transfers between devices with their start and end apart: 2, of which 0 were waited for; matrix products, arithmetic and copies ran while one was open for 0% of the time, Pallas kernels for 24%

profile of v3, /device:TPU:0, one launch (start us, length us, event | category | flops | bytes accessed | tf_op | source)
XLA Modules:
  0.0 74.6 jit_solution(763740329260471111)
XLA Ops:
  0.6 0.0 copy-start.4
  0.6 0.0 copy-start.2
  0.7 0.0 copy-start.3
  1.3 0.8 %copy.12 = f32[3,1,1,2048]{3,0,1,2:T(4,128)S(1)} copy(f32[3,1,1,2048]{3,2,1,0:T(1,128)} %param.11) | data formatting | bytes 49152
  2.1 5.3 %moments.1 = (f32[512,256]{1,0:T(8,128)}, f32[512,768]{1,0:T(8,128)}) custom-call(f32[19,8,64,256]{3,2,1,0:T(8,128)} %pops_ref.5), custom_call_target="tpu_custom_call" | custom-call | tf_op jit(solution)/shard_map/moments/pallas_call | solution.py:598
  7.4 0.0 copy-done.4
  7.5 0.0 copy-done.2
  7.5 0.0 copy-done.3
  7.5 0.7 concatenate.3.pack_ref
  8.2 20.1 %gather.1 = (f32[8,128]{1,0:T(8,128)}, f32[16,2048]{1,0:T(8,128)}) custom-call(f32[512,768]{1,0:T(8,128)} %get-tuple-element.22.velocity_ref, f32[8,2048]{1,0:T(8,128)} %concatenate.3.pack_ref), custom_call_target="tpu_custom_call" | custom-call | tf_op jit(solution)/shard_map/gather/pallas_call | solution.py:608
  28.3 12.9 %total.1.sums_ref = f32[8,128]{1,0:T(8,128)} custom-call(f32[8,128]{1,0:T(8,128)} %get-tuple-element.23.part_ref), custom_call_target="tpu_custom_call" | custom-call | tf_op jit(solution)/shard_map/total/pallas_call | solution.py:630
  41.3 7.7 %spread.1 = (f32[512,768]{1,0:T(8,128)}, f32[3,3]{1,0:T(4,128)}, f32[5,64,256]{2,1,0:T(8,128)}, f32[5,64,256]{2,1,0:T(8,128)}, f32[5,8,256]{2,1,0:T(8,128)}, /*i...) custom-call(f32[1,3]{1,0:T(1,128)} %bitcast.15, ...), custom_call_target="tpu_custom_call" | custom-call | tf_op jit(solution)/shard_map/spread/pallas_call | solution.py:650
  49.0 1.6 %collective-permute-start = (f32[5,64,256]{2,1,0:T(8,128)}, f32[5,64,256]{2,1,0:T(8,128)S(1)}, u32[]{:S(2)}, u32[]{:S(2)}) collective-permute-start(f32[5,64,256]{2,1,0:T(8,128)} %get-tuple-element.27), channel_id=1, source_target_pairs={{0,4},{1,5},{2,6},{3,7},{4,8},{5,9},{6,10},{7,11},{8,12},{9,13},{1... | collective-permute-start | bytes 983048 | tf_op jit(solution)/shard_map/ppermute | solution.py:571
  50.5 3.2 %collective-permute-start.1 = (f32[5,64,256]{2,1,0:T(8,128)}, f32[5,64,256]{2,1,0:T(8,128)S(1)}, u32[]{:S(2)}, u32[]{:S(2)}) collective-permute-start(f32[5,64,256]{2,1,0:T(8,128)} %get-tuple-element.28), channel_id=1, source_target_pairs={{0,28},{1,29},{2,30},{3,31},{4,0},{5,1},{6,2},{7,3},{8,4},{9,5},{1... | collective-permute-start | bytes 983048 | tf_op jit(solution)/shard_map/ppermute | solution.py:571
  53.8 9.5 %collide.1.refs_6_.whole_ref = f32[19,8,64,256]{3,2,1,0:T(8,128)} custom-call(f32[19,8,64,256]{3,2,1,0:T(8,128)} %pops_ref.5, f32[512,768]{1,0:T(8,128)} %get-tuple-element.26.velocity_ref, f32[512,256]{1,0:T(8,128)} %get-tuple-element.25.density_ref), custom_call_target="tpu_custom_call" | custom-call | flops 100000000 | bytes 20000000 | tf_op jit(solution)/shard_map/collide/pallas_call | solution.py:681
  63.3 8.2 %trade.1 = (f32[5,8,256]{2,1,0:T(8,128)}, f32[5,8,256]{2,1,0:T(8,128)}, f32[1,256]{1,0:T(1,128)}, f32[1,256]{1,0:T(1,128)}, f32[1,256]{1,0:T(1,128)}, /*index=5*/f32[1,256]{1,0:T(1,128)}) custom-call(f32[5,8,256]{2,1,0:T(8,128)} %get-tuple-element.29.refs_0_, f32[5,8,256]{2,1,0:T(8,128)} %get-tuple-element.30.refs_1_, f32[1,256]{1,0:T(1,128)} %get-tuple-element.31.refs_2_, ...), custom_call_target="tpu_custom_call" | custom-call | flops 20000000 | bytes 1000000 | tf_op jit(solution)/shard_map/trade/pallas_call | solution.py:698
  71.5 0.0 collective-permute-done.x_low
  71.5 0.0 copy-start
  71.5 0.0 collective-permute-done.1.x_high
  71.5 0.0 copy-start.1
  71.5 0.7 copy-done
  72.2 0.1 copy-done.1
  72.4 2.3 %edges.1 = f32[19,8,64,256]{3,2,1,0:T(8,128)} custom-call(f32[19,8,64,256]{3,2,1,0:T(8,128)} %collide.1.refs_6_.whole_ref, f32[5,64,256]{2,1,0:T(8,128)} %copy-done, f32[5,64,256]{2,1,0:T(8,128)} %copy-done.1, f32[5,8,256]{2,1,0:T(8,128)} %get-tuple-element.35.y_low, f32[5,8,256]{2,1,0:T(8,128)} %get-tuple-element.36.y_high, ...), custom_call_target="tpu_custom_call", output_to_operand_aliasing={{}: (0, {})} | custom-call | tf_op jit(solution)/shard_map/edges/pallas_call | solution.py:708
  (3 shorter events, 0.0 us)
Async XLA Ops:
  0.6 6.8 %copy-start.4 = (f32[1,1,2048]{2,1,0:T(1,128)S(1)}, f32[1,1,2048]{2,1,0:T(1,128)}, u32[]{:S(2)}) copy-start(f32[1,1,2048]{2,1,0:T(1,128)} %param.12) | copy-start | bytes 24580
  0.6 6.8 %copy-start.2 = (s32[3,1,1,2048]{3,2,1,0:T(1,128)S(1)}, s32[3,1,1,2048]{3,2,1,0:T(1,128)}, u32[]{:S(2)}) copy-start(s32[3,1,1,2048]{3,2,1,0:T(1,128)} %param.9) | copy-start | bytes 73732
  0.7 6.9 %copy-start.3 = (f32[1,1,2048]{2,1,0:T(1,128)S(1)}, f32[1,1,2048]{2,1,0:T(1,128)}, u32[]{:S(2)}) copy-start(f32[1,1,2048]{2,1,0:T(1,128)} %param.13) | copy-start | bytes 24580
  49.0 22.5 %collective-permute-start = (f32[5,64,256]{2,1,0:T(8,128)}, f32[5,64,256]{2,1,0:T(8,128)S(1)}, u32[]{:S(2)}, u32[]{:S(2)}) collective-permute-start(f32[5,64,256]{2,1,0:T(8,128)} %get-tuple-element.27), channel_id=1, source_target_pairs={{0,4},{1,5},{2,6},{3,7},{4,8},{5,9},{6,10},{7,11},{8,12},{9,13},{1... | collective-permute-start | bytes 983048 | tf_op jit(solution)/shard_map/ppermute | solution.py:571
  50.5 21.0 %collective-permute-start.1 = (f32[5,64,256]{2,1,0:T(8,128)}, f32[5,64,256]{2,1,0:T(8,128)S(1)}, u32[]{:S(2)}, u32[]{:S(2)}) collective-permute-start(f32[5,64,256]{2,1,0:T(8,128)} %get-tuple-element.28), channel_id=1, source_target_pairs={{0,28},{1,29},{2,30},{3,31},{4,0},{5,1},{6,2},{7,3},{8,4},{9,5},{1... | collective-permute-start | bytes 983048 | tf_op jit(solution)/shard_map/ppermute | solution.py:571
  71.5 0.7 copy-start
  71.5 0.8 %copy-start.1 = (f32[5,64,256]{2,1,0:T(8,128)}, f32[5,64,256]{2,1,0:T(8,128)S(1)}, u32[]{:S(2)}) copy-start(f32[5,64,256]{2,1,0:T(8,128)S(1)} %collective-permute-done.1.x_high) | copy-start | bytes 983044
